TPU v7x, 32 devices: a whole 2x2x4 slice. The times are simulated.
32 devices in a mesh: dp: 2 (over x), fsdp: 4 (over y, core), tensor: 4 (over z).
Axes of the slice: x: 2, y: 2, z: 4, core: 2. Of those that a mesh axis runs over, the one named last changes fastest.
Arguments:
- hidden: bfloat16 [4096, 2048], P(('dp', 'fsdp'), 'tensor'), may hold values from -8 to 8
- norm_gain: bfloat16 [2048], P('tensor'), may hold values from 0.099609375 to 1.8984375
- head_weight: bfloat16 [2048, 32128], P('fsdp', 'tensor'), may hold values from -1 to 1
- token_ids: int32 [8, 512], P(('dp', 'fsdp')), may hold values from 0 to 32127
- lengths: int32 [8], P(('dp', 'fsdp')), may hold values from 128 to 512
- old_logp: float32 [8, 512], P(('dp', 'fsdp')), may hold values from -12.5 to -9.5
- advantages: float32 [8, 512], P(('dp', 'fsdp')), may hold values from -4 to 4
- rollout_logp: float32 [8, 512], P(('dp', 'fsdp'), 'tensor'), may hold values from -16 to -1
- rollout_row: int32 [8], P(('dp', 'fsdp')), may hold values from 0 to 7, each once
Outputs:
- new_logp: float32 [8, 512], P(('dp', 'fsdp'))
- token_loss: float32 [8, 512], P(('dp', 'fsdp'))
- summary: float32 [3], replicated
Inputs may be any that keep to these rules, and one draw needn't show every extreme that they name: `rollout_row`: every row 0 to 7 is named once.
All inputs are finite; a program needn't handle non-finite values.
Results may differ from a plain program's by a relative error of at most 0.0005.
The roundings to bfloat16 on the way count: a program that leaves them out, or rounds other values in their place, can miss the bound.
Values may be sent and summed in bfloat16 or wider, within the bound.
A program may use at most 128 MiB of HBM per device.

v0:
```python
import jax
import jax.numpy as jnp
from jax import lax
from jax.sharding import PartitionSpec as P

clip_eps = 0.2
kl_coef = 0.2
log_limit = 10.0
norm_eps = 1e-06


def combined_all(value, axis, join):
    pieces = jax.tree.map(lambda part: lax.all_gather(part, axis), value)
    head = jax.tree.map(lambda part: part[0], pieces)
    tail = jax.tree.map(lambda part: part[1:], pieces)
    so_far, _ = lax.scan(lambda so_far, section: (join(so_far, section), None), head, tail)
    return so_far


def token_terms(new_logp, old_logp, advantages, ref_logp, live_mask, prob_square):
    shift = new_logp - old_logp
    prob_ratio = jnp.exp(jnp.clip(shift, -log_limit, log_limit))
    clipped = jnp.clip(prob_ratio, 1.0 - clip_eps, 1.0 + clip_eps)
    plain_term = prob_ratio * advantages
    bounded_term = clipped * advantages
    surrogate = jnp.minimum(plain_term, bounded_term)
    ref_gap = ref_logp - new_logp
    gap_clip = jnp.clip(ref_gap, -log_limit, log_limit)
    kl_term = jnp.exp(gap_clip) - gap_clip - 1.0
    token_loss = live_mask * (kl_coef * kl_term - surrogate)
    inside_gap = (jnp.abs(ref_gap) < log_limit).astype(jnp.float32)
    inside_ratio = (jnp.abs(shift) < log_limit).astype(jnp.float32)
    active_term = (plain_term <= bounded_term).astype(jnp.float32)
    grad_coef = live_mask * (
        kl_coef * (1.0 - jnp.exp(gap_clip)) * inside_gap
        - advantages * prob_ratio * active_term * inside_ratio
    )
    grad_square = grad_coef * grad_coef * (prob_square - 2.0 * jnp.exp(new_logp) + 1.0)
    return (token_loss, live_mask * kl_term, grad_square)


def join_stats(earlier, later):
    row_max = jnp.maximum(earlier[0], later[0])
    left_scale = jnp.exp(earlier[0] - row_max)
    right_scale = jnp.exp(later[0] - row_max)
    exp_sum = earlier[1] * left_scale + later[1] * right_scale
    exp_square = earlier[2] * left_scale * left_scale + later[2] * right_scale * right_scale
    return (row_max, exp_sum, exp_square, earlier[3] + later[3])


def exp_sums(logits, row_max):
    shifted = jnp.exp(logits - row_max[:, None])
    return (jnp.sum(shifted, axis=1), jnp.sum(shifted * shifted, axis=1))


def vocab_stats(logits, flat_ids, col_start):
    col_ids = lax.broadcasted_iota(jnp.int32, logits.shape, 1) + col_start
    picked = jnp.sum(jnp.where(col_ids == flat_ids[:, None], logits, 0.0), axis=1)
    local_max = jnp.max(logits, axis=1)
    row_max = lax.pmax(local_max, "tensor")
    exp_sum, exp_square = exp_sums(logits, row_max)
    exp_sum, exp_square, picked = lax.psum((exp_sum, exp_square, picked), "tensor")
    return (row_max, exp_sum, exp_square, picked)


def shards(
    hidden,
    norm_gain,
    head_weight,
    token_ids,
    lengths,
    old_logp,
    advantages,
    rollout_logp,
    rollout_row,
):
    tok_rows = hidden.shape[0]
    full_rows, full_gain = (
        lax.all_gather(hidden, "tensor", axis=1, tiled=True),
        lax.all_gather(norm_gain, "tensor", axis=0, tiled=True),
    )
    values = full_rows.astype(jnp.float32)
    inv_rms = lax.rsqrt(jnp.mean(values * values, axis=1, keepdims=True) + norm_eps)
    normed = (values * inv_rms * full_gain.astype(jnp.float32)[None, :]).astype(jnp.bfloat16)
    flat_ids = token_ids.reshape(-1)
    vocab_cols = head_weight.shape[1]
    tensor_pos = lax.axis_index("tensor")
    half_cols = vocab_cols // 2
    dp_pos = lax.axis_index("dp")
    own_cols = lax.dynamic_slice_in_dim(head_weight, dp_pos * half_cols, half_cols, 1)
    pair_rows = lax.all_gather(normed, "dp", axis=0, tiled=True)
    pair_ids = lax.all_gather(flat_ids, "dp", axis=0, tiled=True)
    logits = jnp.dot(
        pair_rows,
        lax.all_gather(own_cols, "fsdp", axis=0, tiled=True),
        preferred_element_type=jnp.float32,
    )
    soft_stats = vocab_stats(logits, pair_ids, tensor_pos * vocab_cols + dp_pos * half_cols)
    soft_stats = combined_all(soft_stats, "dp", join_stats)
    soft_stats = tuple(
        (lax.dynamic_slice_in_dim(member, dp_pos * tok_rows, tok_rows, 0) for member in soft_stats)
    )
    row_max, exp_sum, exp_square, picked = soft_stats
    new_logp = (picked - row_max - jnp.log(exp_sum)).reshape(token_ids.shape)
    prob_square = (exp_square / (exp_sum * exp_sum)).reshape(token_ids.shape)
    ref_all = lax.all_gather(rollout_logp, ("dp", "fsdp"), axis=0, tiled=True)
    own_ref = jnp.take(ref_all, rollout_row, axis=0)
    ref_logp = lax.all_gather(own_ref, "tensor", axis=1, tiled=True)
    positions = lax.broadcasted_iota(jnp.int32, token_ids.shape, 1)
    live_mask = (positions < lengths[:, None]).astype(jnp.float32)
    token_loss, kl_part, grad_part = token_terms(
        new_logp, old_logp, advantages, ref_logp, live_mask, prob_square
    )
    live_count, loss_sum, kl_sum, grad_sum = lax.psum(
        (jnp.sum(live_mask), jnp.sum(token_loss), jnp.sum(kl_part), jnp.sum(grad_part)),
        ("dp", "fsdp"),
    )
    summary = jnp.stack(
        [loss_sum / live_count, kl_sum / live_count, jnp.sqrt(grad_sum / live_count)]
    )
    return (new_logp, token_loss, summary)


def solution(mesh):
    in_specs = (
        P(("dp", "fsdp"), "tensor"),
        P("tensor"),
        P("fsdp", "tensor"),
        P(("dp", "fsdp"), None),
        P(("dp", "fsdp")),
        P(("dp", "fsdp"), None),
        P(("dp", "fsdp"), None),
        P(("dp", "fsdp"), "tensor"),
        P(("dp", "fsdp")),
    )
    out_specs = (P(("dp", "fsdp"), None), P(("dp", "fsdp"), None), P())
    return jax.shard_map(shards, mesh=mesh, in_specs=in_specs, out_specs=out_specs, check_vma=False)
```

profile of v0, /device:TPU:0, one launch (start us, length us, event | category | flops | bytes accessed | tf_op | source)
XLA Modules:
  0.0 327.2 jit_solution(12771580866404278968)
XLA Ops:
  7.2 0.0 all-gather.11.cloned.1.call-start
  7.2 0.7 all-gather.11.cloned.1.call-update
  7.9 0.0 all-gather.13.cloned.1.call-start
  7.9 0.7 reshape.90
  8.6 13.6 %all-gather.2 = bf16[4,1,512]{2,1,0:T(2,128)(2,1)S(1)} all-gather(bf16[1,1,512]{2,1,0:T(2,128)(2,1)S(1)} %reshape.90), channel_id=1, replica_groups=mesh['dp'=2,'fsdp'=4,'tensor'=4] {'tensor'}, dimensions={0}, use_global_device_ids=true | all-gather | bytes 5120 | tf_op jit(solution)/shard_map/all_gather | solution.py:80
  22.3 35.7 %all-gather.11.cloned.1.call-done = bf16[512,2048]{1,0:T(8,128)(2,1)} async-done(((bf16[512,512]{1,0:T(8,128)(2,1)}), bf16[512,2048]{1,0:T(8,128)(2,1)}) %all-gather.11.cloned.1.call-update) | async-done | bytes 2097168 | tf_op jit(solution)/shard_map/all_gather | solution.py:79
  58.0 2.1 fusion.1
  60.0 3.5 %fusion.3 = bf16[512,2048]{1,0:T(8,128)(2,1)} fusion(bf16[512,2048]{1,0:T(8,128)(2,1)} %all-gather.11.cloned.1.call-done, f32[2048]{0:T(1024)S(1)} %bitcast.29, f32[512]{0:T(512)S(1)} %add_rsqrt_fusion), kind=kLoop, calls=%fused_computation.8 | loop fusion | flops 4194304 | bytes 4204544 | tf_op jit(solution)/shard_map/convert_element_type | solution.py:84
  63.5 0.0 all-gather.13.cloned.1.call-update
  63.5 0.0 all-gather.15.cloned.1.call-start
  63.6 0.0 copy-start.4
  63.6 0.0 copy-start.1
  63.6 4.4 %constant_dynamic-slice_fusion.1 = bf16[512,4016]{0,1:T(8,128)(2,1)} fusion(bf16[512,8032]{0,1:T(8,128)(2,1)} %param.11, s32[]{:T(128)S(6)} %select_n.30), kind=kLoop, calls=%fused_computation.37 | loop fusion | bytes 8224772 | tf_op jit(solution)/shard_map/dynamic_slice | solution.py:90
  68.0 0.0 all-gather.15.cloned.1.call-update
  69.3 0.6 convert_reduce_fusion
  70.0 0.0 copy-done.4
  70.0 8.9 %all-gather.5 = f32[8,1,128]{2,1,0:T(1,128)S(1)} all-gather(f32[1,1,128]{2,1,0:T(1,128)S(1)} %bitcast.45), channel_id=1, replica_groups=mesh['dp'=2,'fsdp'=4,'tensor'=4] {'dp','fsdp'}, dimensions={0}, use_global_device_ids=true | all-gather | bytes 4608 | tf_op jit(solution)/shard_map/all_gather | solution.py:106
  78.8 8.6 %all_gather.57 = f32[1,512]{1,0:T(1,128)S(1)} all-gather(f32[1,128]{1,0:T(1,128)S(1)} %fusion.8), channel_id=1, replica_groups=mesh['dp'=2,'fsdp'=4,'tensor'=4] {'tensor'}, dimensions={1}, use_global_device_ids=true | all-gather | bytes 2560 | tf_op jit(solution)/shard_map/all_gather | solution.py:108
  87.4 0.0 copy-done.1
  87.4 4.5 %all-gather = s32[1,1024]{1,0:T(1,128)S(1)} all-gather(s32[1,512]{1,0:T(1,128)S(1)} %copy-done.1), channel_id=2, replica_groups=mesh['dp'=2,'fsdp'=4,'tensor'=4] {'dp'}, dimensions={1}, use_global_device_ids=true | all-gather | bytes 6144 | tf_op jit(solution)/shard_map/all_gather | solution.py:92
  92.0 27.3 %all-gather.13.cloned.1.call-done = bf16[1024,2048]{1,0:T(8,128)(2,1)} async-done(((bf16[512,2048]{1,0:T(8,128)(2,1)}), bf16[1024,2048]{1,0:T(8,128)(2,1)}) %all-gather.13.cloned.1.call-update) | async-done | bytes 4194320 | tf_op jit(solution)/shard_map/all_gather | solution.py:91
  119.3 105.6 %all-gather.15.cloned.1.call-done = bf16[2048,4016]{0,1:T(8,128)(2,1)} async-done(((bf16[512,4016]{0,1:T(8,128)(2,1)}), bf16[2048,4016]{0,1:T(8,128)(2,1)}) %all-gather.15.cloned.1.call-update) | async-done | bytes 16449552 | tf_op jit(solution)/shard_map/all_gather | solution.py:95
  224.9 23.4 %fusion.15 = (f32[1024]{0:T(1024)S(1)}, f32[1024,4016]{0,1:T(8,128)}) fusion(bf16[1024,2048]{1,0:T(8,128)(2,1)} %all-gather.13.cloned.1.call-done, bf16[2048,4016]{0,1:T(8,128)(2,1)} %all-gather.15.cloned.1.call-done), kind=kOutput, calls=%fused_computation.46 | convolution fusion | flops 16848436224 | bytes 37097472 | tf_op jit(solution)/shard_map/dot_general | solution.py:93
  248.3 11.7 %pmax.7 = f32[1024]{0:T(1024)S(1)} all-reduce(f32[1024]{0:T(1024)S(1)} %get-tuple-element.65), channel_id=1, replica_groups=mesh['dp'=2,'fsdp'=4,'tensor'=4] {'tensor'}, use_global_device_ids=true, to_apply=%region_4.5 | all-reduce | flops 1024 | bytes 8192 | tf_op jit(solution)/shard_map/pmax | solution.py:60
  259.9 4.3 %all-gather.1 = f32[2048]{0:T(1024)S(1)} all-gather(f32[1024]{0:T(1024)S(1)} %pmax.7), channel_id=3, replica_groups=mesh['dp'=2,'fsdp'=4,'tensor'=4] {'dp'}, dimensions={0}, use_global_device_ids=true | all-gather | bytes 12288 | tf_op jit(solution)/shard_map/all_gather | solution.py:13
  264.3 0.0 copy-start.2
  264.3 0.0 copy-start.3
  264.3 8.7 %multiply_reduce_fusion = (f32[1024]{0:T(1024)S(1)}, f32[1024]{0:T(1024)S(1)}, f32[1024]{0:T(1024)S(1)}) fusion(f32[1024,4016]{0,1:T(8,128)} %get-tuple-element.66, f32[1024]{0:T(1024)S(1)} %pmax.7, s32[1024]{0:T(1024)S(1)} %bitcast.33, s32[4016]{0:T(1024)S(1)} %iota_add_fusion), kind=kLoop, calls=%fused_computation | loop fusion | flops 28783616 | bytes 16486080 | tf_op jit(solution)/shard_map/reduce_sum | solution.py:53
  273.0 15.5 %all-reduce.1 = (f32[1,1024]{1,0:T(1,128)S(1)}, f32[1,1024]{1,0:T(1,128)S(1)}, f32[1,1024]{1,0:T(1,128)S(1)}) all-reduce(f32[1,1024]{1,0:T(1,128)S(1)} %bitcast.32, f32[1,1024]{1,0:T(1,128)S(1)} %bitcast.31, f32[1,1024]{1,0:T(1,128)S(1)} %bitcast.30), channel_id=1, replica_groups=mesh['dp'=2,'fsdp'=4,'tensor'=4] {'tensor'}, use_global_device_ids=true, to_apply=%region_2.3 | all-reduce | flops 3072 | bytes 24576 | tf_op jit(solution)/shard_map/psum | solution.py:62
  288.5 4.3 %all-gather.3 = f32[2,1,1024]{2,1,0:T(1,128)S(1)} all-gather(f32[1,1,1024]{2,1,0:T(1,128)S(1)} %bitcast.44), channel_id=1, replica_groups=mesh['dp'=2,'fsdp'=4,'tensor'=4] {'dp'}, dimensions={0}, use_global_device_ids=true | all-gather | bytes 12288 | tf_op jit(solution)/shard_map/all_gather | solution.py:13
  292.9 4.3 %all-gather.6 = f32[2,1,1024]{2,1,0:T(1,128)S(1)} all-gather(f32[1,1,1024]{2,1,0:T(1,128)S(1)} %bitcast.43), channel_id=1, replica_groups=mesh['dp'=2,'fsdp'=4,'tensor'=4] {'dp'}, dimensions={0}, use_global_device_ids=true | all-gather | bytes 12288 | tf_op jit(solution)/shard_map/all_gather | solution.py:13
  297.2 4.3 %all-gather.4 = f32[2,1,1024]{2,1,0:T(1,128)S(1)} all-gather(f32[1,1,1024]{2,1,0:T(1,128)S(1)} %bitcast.42), channel_id=1, replica_groups=mesh['dp'=2,'fsdp'=4,'tensor'=4] {'dp'}, dimensions={0}, use_global_device_ids=true | all-gather | bytes 12288 | tf_op jit(solution)/shard_map/all_gather | solution.py:13
  301.6 0.1 subtract_add_fusion
  301.7 0.0 copy-start
  301.7 0.0 copy-done.2
  301.7 0.0 copy-done.3
  301.7 1.3 fusion.10
  303.0 0.7 select_reduce_fusion.1
  303.7 12.5 %all-reduce = (f32[]{:T(128)}, f32[]{:T(128)}, f32[]{:T(128)}, f32[]{:T(128)}) all-reduce(f32[]{:T(128)} %get-tuple-element.58, f32[]{:T(128)} %convert_reduce_fusion, f32[]{:T(128)} %select_reduce_fusion.1, f32[]{:T(128)} %get-tuple-element.51), channel_id=1, replica_groups=mesh['dp'=2,'fsdp'=4,'tensor'=4] {'dp','fsdp'}, use_global_device_ids=true, to_apply=%region_16.17 | all-reduce | flops 4 | bytes 32 | tf_op jit(solution)/shard_map/psum | solution.py:114
  320.1 0.6 pad_maximum_fusion
  320.7 0.0 copy-done
  (10 shorter events, 0.1 us)
Async XLA Ops:
  7.2 50.8 %all-gather.11.cloned.1.call-start = ((), (), s32[]{:S(2)}) async-start(), calls=%async_computation | async-start | bytes 2621440 | tf_op jit(solution)/shard_map/all_gather | solution.py:79
  7.9 111.4 %all-gather.13.cloned.1.call-start = ((), (), s32[]{:S(2)}) async-start(), calls=%async_computation.1 | async-start | bytes 6291456 | tf_op jit(solution)/shard_map/all_gather | solution.py:91
  63.5 161.4 %all-gather.15.cloned.1.call-start = ((), (), s32[]{:S(2)}) async-start(), calls=%async_computation.2 | async-start | bytes 20561920 | tf_op jit(solution)/shard_map/all_gather | solution.py:95
  63.6 6.4 %copy-start.4 = (f32[1,128]{1,0:T(1,128)S(1)}, f32[1,128]{1,0:T(1,128)}, u32[]{:S(2)}) copy-start(f32[1,128]{1,0:T(1,128)} %param.16) | copy-start | bytes 1540
  63.6 23.8 %copy-start.1 = (s32[1,512]{1,0:T(1,128)S(1)}, s32[1,512]{1,0:T(1,128)}, u32[]{:S(2)}) copy-start(s32[1,512]{1,0:T(1,128)} %param.12) | copy-start | bytes 6148
  264.3 37.4 %copy-start.2 = (f32[1,512]{1,0:T(1,128)S(1)}, f32[1,512]{1,0:T(1,128)}, u32[]{:S(2)}) copy-start(f32[1,512]{1,0:T(1,128)} %param.15) | copy-start | bytes 6148
  264.3 37.4 %copy-start.3 = (f32[1,512]{1,0:T(1,128)S(1)}, f32[1,512]{1,0:T(1,128)}, u32[]{:S(2)}) copy-start(f32[1,512]{1,0:T(1,128)} %param.14) | copy-start | bytes 6148
  301.7 19.0 %copy-start = (f32[512]{0:T(512)}, f32[512]{0:T(512)S(1)}, u32[]{:S(2)}) copy-start(f32[512]{0:T(512)S(1)} %get-tuple-element.55) | copy-start | bytes 6148
Sparse Core Ops, SparseCore 0:
  9.5 48.3 all-gather.10
  63.7 55.5 all-gather.12
  120.9 104.0 all-gather.14
where the time goes:
time: 328 us; the launch traced here: 327 us
  waiting for transfers between devices  169 us (52%)
  blocking collectives  92.7 us (28%)
  matrix products  23.4 us (7%)
  between operations  19.1 us (6%)
  other arithmetic  17.5 us (5%)
  local copies, waits for them, and re-layouts  5.08 us (2%)
    all_gather x1, waiting for transfers between devices, shards(): lax.all_gather(own_cols, 'fsdp', axis=0, tiled=True)  106 us
    all_gather x1, waiting for transfers between devices, shards(): lax.all_gather(hidden, 'tensor', axis=1, tiled=True)  35.7 us
    all_gather x1, waiting for transfers between devices, shards(): pair_rows = lax.all_gather(normed, 'dp', axis=0, tiled=True)  27.3 us
    dot_general x1, matrix products, shards(): jnp.dot(pair_rows, lax.all_gather(own_cols, 'fsdp', axis=0, tiled=True),...  23.4 us
    all_gather x4, blocking collectives, combined_all(): pieces = jax.tree.map(lambda part: lax.all_gather(part, axis), value)  17.4 us
    psum x1, blocking collectives, vocab_stats(): lax.psum((exp_sum, exp_square, picked), 'tensor')  15.5 us
    all_gather x1, blocking collectives, shards(): lax.all_gather(norm_gain, 'tensor', axis=0, tiled=True)  13.6 us
    psum x1, blocking collectives, shards(): lax.psum((jnp.sum(live_mask), jnp.sum(token_loss), jnp.sum(kl_part), jnp....  12.5 us
  transfers between devices with their start and end apart: 3, of which 3 were waited for; matrix products, arithmetic and copies ran while one was open for 2% of the time, Pallas kernels for 0%

commit v1 on v0

--- a/solution.py
+++ b/solution.py
@@ -92,7 +92,9 @@
     pair_ids = lax.all_gather(flat_ids, "dp", axis=0, tiled=True)
     logits = jnp.dot(
         pair_rows,
-        lax.all_gather(own_cols, "fsdp", axis=0, tiled=True),
+        jnp.concatenate(
+            lax.all_to_all(jnp.stack([own_cols] * lax.axis_size("fsdp")), "fsdp", 0, 0), axis=0
+        ),
         preferred_element_type=jnp.float32,
     )
     soft_stats = vocab_stats(logits, pair_ids, tensor_pos * vocab_cols + dp_pos * half_cols)

time: 328 us -> 347 us (1.058)
  waiting for transfers between devices: 169 us -> 37.5 us
  blocking collectives: 92.7 us -> 211 us
  local copies, waits for them, and re-layouts: 5.08 us -> 29.3 us
  starting transfers between devices: 0.12 us -> 7.14 us
    all_gather x1, blocking collectives: 8.88 us -> 126 us  [shards(): ref_all = lax.all_gather(rollout_logp, ('dp', 'fsdp'), axis=0, tiled=True)]
    all_gather x1 -> x0, waiting for transfers between devices: 106 us -> none  [shards(): lax.all_gather(own_cols, 'fsdp', axis=0, tiled=True)]
    all_gather x1, waiting for transfers between devices: 27.3 us -> 0.01 us  [shards(): pair_rows = lax.all_gather(normed, 'dp', axis=0, tiled=True)]
    all_to_all x0 -> x1, local copies, waits for them, and re-layouts: none -> 20.7 us  [shards(): lax.all_to_all(jnp.stack([own_cols] * lax.axis_size('fsdp')), 'fsdp', 0, 0)]
    all_to_all x0 -> x1, starting transfers between devices: none -> 7.06 us  [shards(): lax.all_to_all(jnp.stack([own_cols] * lax.axis_size('fsdp')), 'fsdp', 0, 0)]
    another operation x0 -> x1, local copies, waits for them, and re-layouts: none -> 6.14 us  [shards(): jnp.stack([own_cols] * lax.axis_size('fsdp'))]
  transfers between devices with their start and end apart: 3 -> 3, of which waited for: 3 -> 1; matrix products, arithmetic and copies ran while one was open for 2% -> 8% of each run, Pallas kernels for 0% -> 0%
where the time goes in v1:
time: 347 us; the launch traced here: 345 us
  blocking collectives  211 us (61%)
  waiting for transfers between devices  37.5 us (11%)
  local copies, waits for them, and re-layouts  29.3 us (8%)
  matrix products  23.7 us (7%)
  between operations  19.6 us (6%)
  other arithmetic  17.5 us (5%)
  starting transfers between devices  7.14 us (2%)
    all_gather x1, blocking collectives, shards(): ref_all = lax.all_gather(rollout_logp, ('dp', 'fsdp'), axis=0, tiled=True)  126 us
    all_gather x1, waiting for transfers between devices, shards(): lax.all_gather(hidden, 'tensor', axis=1, tiled=True)  36.8 us
    dot_general x1, matrix products, shards(): jnp.dot(pair_rows, jnp.concatenate(lax.all_to_all(jnp.stack([own_cols] *...  23.7 us
    all_to_all x1, local copies, waits for them, and re-layouts, shards(): lax.all_to_all(jnp.stack([own_cols] * lax.axis_size('fsdp')), 'fsdp', 0, 0)  20.7 us
    all_gather x4, blocking collectives, combined_all(): pieces = jax.tree.map(lambda part: lax.all_gather(part, axis), value)  17.4 us
    psum x1, blocking collectives, vocab_stats(): lax.psum((exp_sum, exp_square, picked), 'tensor')  17.4 us
    all_gather x1, blocking collectives, shards(): lax.all_gather(norm_gain, 'tensor', axis=0, tiled=True)  13.6 us
    psum x1, blocking collectives, shards(): lax.psum((jnp.sum(live_mask), jnp.sum(token_loss), jnp.sum(kl_part), jnp....  12.5 us
  transfers between devices with their start and end apart: 3, of which 1 were waited for; matrix products, arithmetic and copies ran while one was open for 8% of the time, Pallas kernels for 0%

profile of v1, /device:TPU:0, one launch (start us, length us, event | category | flops | bytes accessed | tf_op | source)
XLA Modules:
  0.0 345.5 jit_solution(3509443657696746799)
XLA Ops:
  7.2 2.4 constant_dynamic-slice_fusion.1
  9.6 6.1 %stack.19 = bf16[4,512,4016]{1,2,0:T(8,128)(2,1)} broadcast(bf16[512,4016]{0,1:T(8,128)(2,1)S(1)} %constant_dynamic-slice_fusion.1), dimensions={1,2} | broadcast | bytes 20561920 | tf_op jit(solution)/shard_map/stack | solution.py:96
  15.7 0.0 copy-start.4
  15.7 7.1 %all-to-all-start = ((bf16[4,512,4016]{1,2,0:T(8,128)(2,1)}), bf16[4,512,4016]{1,2,0:T(8,128)(2,1)}, u32[]{:S(2)}, u32[]{:S(2)}) async-start(bf16[4,512,4016]{1,2,0:T(8,128)(2,1)} %stack.19), calls=%async_computation | async-start | bytes 32899072 | tf_op jit(solution)/shard_map/all_to_all | solution.py:96
  22.8 0.0 copy-start.5
  22.8 0.0 copy-start.1
  22.8 0.0 all-gather.10.cloned.1.call-start
  22.9 0.7 all-gather.10.cloned.1.call-update
  23.6 0.0 all-gather.12.cloned.1.call-start
  23.6 0.0 copy-done.4
  23.6 13.6 %all-gather.2 = bf16[4,1,512]{2,1,0:T(2,128)(2,1)S(1)} all-gather(bf16[1,1,512]{2,1,0:T(2,128)(2,1)S(1)} %reshape.96), channel_id=1, replica_groups=mesh['dp'=2,'fsdp'=4,'tensor'=4] {'tensor'}, dimensions={0}, use_global_device_ids=true | all-gather | bytes 5120 | tf_op jit(solution)/shard_map/all_gather | solution.py:80
  37.3 36.8 %all-gather.10.cloned.1.call-done = bf16[512,2048]{1,0:T(8,128)(2,1)} async-done(((bf16[512,512]{1,0:T(8,128)(2,1)}), bf16[512,2048]{1,0:T(8,128)(2,1)}) %all-gather.10.cloned.1.call-update) | async-done | bytes 2097168 | tf_op jit(solution)/shard_map/all_gather | solution.py:79
  74.1 2.1 fusion.1
  76.1 3.4 fusion.3
  79.6 0.0 all-gather.12.cloned.1.call-update
  80.9 0.7 convert_reduce_fusion
  81.6 0.0 copy-done.5
  81.6 126.1 %all-gather.5 = f32[8,1,128]{2,1,0:T(1,128)S(1)} all-gather(f32[1,1,128]{2,1,0:T(1,128)S(1)} %bitcast.47), channel_id=1, replica_groups=mesh['dp'=2,'fsdp'=4,'tensor'=4] {'dp','fsdp'}, dimensions={0}, use_global_device_ids=true | all-gather | bytes 4608 | tf_op jit(solution)/shard_map/all_gather | solution.py:108
  207.7 11.1 %all_gather.53 = f32[1,512]{1,0:T(1,128)S(1)} all-gather(f32[1,128]{1,0:T(1,128)S(1)} %fusion.8), channel_id=1, replica_groups=mesh['dp'=2,'fsdp'=4,'tensor'=4] {'tensor'}, dimensions={1}, use_global_device_ids=true | all-gather | bytes 2560 | tf_op jit(solution)/shard_map/all_gather | solution.py:110
  218.9 0.0 copy-done.1
  218.9 4.4 %all-gather = s32[1,1024]{1,0:T(1,128)S(1)} all-gather(s32[1,512]{1,0:T(1,128)S(1)} %copy-done.1), channel_id=2, replica_groups=mesh['dp'=2,'fsdp'=4,'tensor'=4] {'dp'}, dimensions={1}, use_global_device_ids=true | all-gather | bytes 6144 | tf_op jit(solution)/shard_map/all_gather | solution.py:92
  223.2 0.0 all-to-all-done
  223.2 20.7 %copy.13 = bf16[4,512,4016]{2,1,0:T(8,128)(2,1)} copy(bf16[4,512,4016]{1,2,0:T(8,128)(2,1)} %all-to-all-done) | data formatting | bytes 32899072 | tf_op jit(solution)/shard_map/all_to_all | solution.py:96
  243.9 0.0 all-gather.12.cloned.1.call-done
  243.9 23.7 %fusion.15 = (f32[1024]{0:T(1024)S(1)}, f32[1024,4016]{0,1:T(8,128)}) fusion(bf16[1024,2048]{1,0:T(8,128)(2,1)} %all-gather.12.cloned.1.call-done, bf16[2048,4016]{1,0:T(8,128)(2,1)} %bitcast.30), kind=kOutput, calls=%fused_computation.46 | convolution fusion | flops 16848436224 | bytes 37097472 | tf_op jit(solution)/shard_map/dot_general | solution.py:93
  267.6 8.3 %pmax.7 = f32[1024]{0:T(1024)S(1)} all-reduce(f32[1024]{0:T(1024)S(1)} %get-tuple-element.65), channel_id=1, replica_groups=mesh['dp'=2,'fsdp'=4,'tensor'=4] {'tensor'}, use_global_device_ids=true, to_apply=%region_4.5 | all-reduce | flops 1024 | bytes 8192 | tf_op jit(solution)/shard_map/pmax | solution.py:60
  275.9 4.3 %all-gather.1 = f32[2048]{0:T(1024)S(1)} all-gather(f32[1024]{0:T(1024)S(1)} %pmax.7), channel_id=3, replica_groups=mesh['dp'=2,'fsdp'=4,'tensor'=4] {'dp'}, dimensions={0}, use_global_device_ids=true | all-gather | bytes 12288 | tf_op jit(solution)/shard_map/all_gather | solution.py:13
  280.3 0.0 copy-start.2
  280.3 0.0 copy-start.3
  280.3 8.7 %multiply_reduce_fusion = (f32[1024]{0:T(1024)S(1)}, f32[1024]{0:T(1024)S(1)}, f32[1024]{0:T(1024)S(1)}) fusion(f32[1024,4016]{0,1:T(8,128)} %get-tuple-element.66, f32[1024]{0:T(1024)S(1)} %pmax.7, s32[1024]{0:T(1024)S(1)} %bitcast.35, s32[4016]{0:T(1024)S(1)} %iota_add_fusion), kind=kLoop, calls=%fused_computation | loop fusion | flops 28783616 | bytes 16486080 | tf_op jit(solution)/shard_map/reduce_sum | solution.py:53
  289.0 17.4 %all-reduce.1 = (f32[1,1024]{1,0:T(1,128)S(1)}, f32[1,1024]{1,0:T(1,128)S(1)}, f32[1,1024]{1,0:T(1,128)S(1)}) all-reduce(f32[1,1024]{1,0:T(1,128)S(1)} %bitcast.34, f32[1,1024]{1,0:T(1,128)S(1)} %bitcast.33, f32[1,1024]{1,0:T(1,128)S(1)} %bitcast.32), channel_id=1, replica_groups=mesh['dp'=2,'fsdp'=4,'tensor'=4] {'tensor'}, use_global_device_ids=true, to_apply=%region_2.3 | all-reduce | flops 3072 | bytes 24576 | tf_op jit(solution)/shard_map/psum | solution.py:62
  306.3 4.3 %all-gather.3 = f32[2,1,1024]{2,1,0:T(1,128)S(1)} all-gather(f32[1,1,1024]{2,1,0:T(1,128)S(1)} %bitcast.46), channel_id=1, replica_groups=mesh['dp'=2,'fsdp'=4,'tensor'=4] {'dp'}, dimensions={0}, use_global_device_ids=true | all-gather | bytes 12288 | tf_op jit(solution)/shard_map/all_gather | solution.py:13
  310.7 4.3 %all-gather.6 = f32[2,1,1024]{2,1,0:T(1,128)S(1)} all-gather(f32[1,1,1024]{2,1,0:T(1,128)S(1)} %bitcast.45), channel_id=1, replica_groups=mesh['dp'=2,'fsdp'=4,'tensor'=4] {'dp'}, dimensions={0}, use_global_device_ids=true | all-gather | bytes 12288 | tf_op jit(solution)/shard_map/all_gather | solution.py:13
  315.0 4.3 %all-gather.4 = f32[2,1,1024]{2,1,0:T(1,128)S(1)} all-gather(f32[1,1,1024]{2,1,0:T(1,128)S(1)} %bitcast.44), channel_id=1, replica_groups=mesh['dp'=2,'fsdp'=4,'tensor'=4] {'dp'}, dimensions={0}, use_global_device_ids=true | all-gather | bytes 12288 | tf_op jit(solution)/shard_map/all_gather | solution.py:13
  319.4 0.1 subtract_add_fusion
  319.5 0.0 copy-start
  319.5 0.0 copy-done.2
  319.5 0.0 copy-done.3
  319.5 1.3 fusion.10
  320.8 0.7 select_reduce_fusion.1
  321.5 12.5 %all-reduce = (f32[]{:T(128)}, f32[]{:T(128)}, f32[]{:T(128)}, f32[]{:T(128)}) all-reduce(f32[]{:T(128)} %get-tuple-element.58, f32[]{:T(128)} %convert_reduce_fusion, f32[]{:T(128)} %select_reduce_fusion.1, f32[]{:T(128)} %get-tuple-element.51), channel_id=1, replica_groups=mesh['dp'=2,'fsdp'=4,'tensor'=4] {'dp','fsdp'}, use_global_device_ids=true, to_apply=%region_16.17 | all-reduce | flops 4 | bytes 32 | tf_op jit(solution)/shard_map/psum | solution.py:116
  338.1 0.6 pad_maximum_fusion
  338.7 0.0 copy-done
  (11 shorter events, 0.1 us)
Async XLA Ops:
  15.7 7.9 %copy-start.4 = (bf16[512]{0:T(512)(128)(2,1)S(1)}, bf16[512]{0:T(512)(128)(2,1)}, u32[]{:S(2)}) copy-start(bf16[512]{0:T(512)(128)(2,1)} %param.10) | copy-start | bytes 3076
  15.7 207.5 %all-to-all-start = ((bf16[4,512,4016]{1,2,0:T(8,128)(2,1)}), bf16[4,512,4016]{1,2,0:T(8,128)(2,1)}, u32[]{:S(2)}, u32[]{:S(2)}) async-start(bf16[4,512,4016]{1,2,0:T(8,128)(2,1)} %stack.19), calls=%async_computation | async-start | bytes 32899072 | tf_op jit(solution)/shard_map/all_to_all | solution.py:96
  22.8 58.8 %copy-start.5 = (f32[1,128]{1,0:T(1,128)S(1)}, f32[1,128]{1,0:T(1,128)}, u32[]{:S(2)}) copy-start(f32[1,128]{1,0:T(1,128)} %param.16) | copy-start | bytes 1540
  22.8 196.0 %copy-start.1 = (s32[1,512]{1,0:T(1,128)S(1)}, s32[1,512]{1,0:T(1,128)}, u32[]{:S(2)}) copy-start(s32[1,512]{1,0:T(1,128)} %param.12) | copy-start | bytes 6148
  22.8 51.2 %all-gather.10.cloned.1.call-start = ((), (), s32[]{:S(2)}) async-start(), calls=%async_computation.1 | async-start | bytes 2621440 | tf_op jit(solution)/shard_map/all_gather | solution.py:79
  23.6 220.4 %all-gather.12.cloned.1.call-start = ((), (), s32[]{:S(2)}) async-start(), calls=%async_computation.2 | async-start | bytes 6291456 | tf_op jit(solution)/shard_map/all_gather | solution.py:91
  280.3 39.2 %copy-start.2 = (f32[1,512]{1,0:T(1,128)S(1)}, f32[1,512]{1,0:T(1,128)}, u32[]{:S(2)}) copy-start(f32[1,512]{1,0:T(1,128)} %param.15) | copy-start | bytes 6148
  280.3 39.2 %copy-start.3 = (f32[1,512]{1,0:T(1,128)S(1)}, f32[1,512]{1,0:T(1,128)}, u32[]{:S(2)}) copy-start(f32[1,512]{1,0:T(1,128)} %param.14) | copy-start | bytes 6148
  319.5 19.2 %copy-start = (f32[512]{0:T(512)}, f32[512]{0:T(512)S(1)}, u32[]{:S(2)}) copy-start(f32[512]{0:T(512)S(1)} %get-tuple-element.55) | copy-start | bytes 6148
Sparse Core Ops, SparseCore 0:
  25.2 48.7 all-gather.9
  79.7 55.5 all-gather.11
